TPU v7x, 32 devices: a whole 2x2x4 slice. The times are simulated.
32 devices in a mesh: head: 2 (over y), outer: 4 (over z), inner: 4 (over x, core).
Axes of the slice: x: 2, y: 2, z: 4, core: 2. Of those that a mesh axis runs over, the one named last changes fastest.
Arguments:
- queries: bfloat16 [1024, 2048], P('outer', ('head', 'inner')), may hold values from -100 to 100
- keys: bfloat16 [1024, 256], P('outer', 'head'), may hold values from -5 to 5
- values: bfloat16 [1024, 256], P('outer', 'head'), may hold values from -6 to 6
- grad_out: bfloat16 [1024, 2048], P('outer', ('head', 'inner')), may hold values from -24 to 24
- hidden_in: bfloat16 [1024, 8192], P('outer', ('head', 'inner')), may hold values from -6 to 6
- adapter_a: bfloat16 [8192, 16], P(('head', 'inner')), may hold values from -0.0625 to 0.0625
- adapter_b: bfloat16 [16, 256], P(None, 'head'), may hold values from -1.5 to 1.5
- block_order: int32 [8], replicated, may hold values from 0 to 7, each once
- doc_ids: int32 [1024], replicated, may hold values from 0 to 3, never falling along the last dimension, each value on 1 to 512 neighbouring positions
Outputs:
- grad_query: bfloat16 [1024, 2048], P('outer', ('head', 'inner'))
- grad_key: bfloat16 [1024, 256], P('outer', 'head')
- grad_value: bfloat16 [1024, 256], P('outer', 'head')
- grad_a: float32 [8192, 16], P(('head', 'inner'))
- grad_b: float32 [16, 256], P(None, 'head')
Inputs may be any that keep to these rules, and one draw needn't show every extreme that they name: `block_order`: a permutation of the stored blocks. `doc_ids`: never falling along positions; each document has 1 to 512 positions.
All inputs are finite; a program needn't handle non-finite values.
Results may differ from a plain program's by a relative error of at most 0.024.
Values may be sent and summed in bfloat16 or wider, within the bound.
A program may use at most 64 MiB of HBM per device.

v0:
```python
import jax
import jax.numpy as jnp
from jax import lax
from jax.sharding import PartitionSpec as P

HEAD_DIM = 128


NEGATIVE = -1e30


def passed_along(value, axis, steps):
    count = lax.axis_size(axis)
    pairs = [(source, (source + steps) % count) for source in range(count)]
    return lax.ppermute(value, axis, pairs)


def block_meta(block_table, doc_table, block_id, half_rows):
    first_pos = block_table[block_id] * half_rows
    places = first_pos + jnp.arange(half_rows, dtype=jnp.int32)
    owners = lax.dynamic_slice_in_dim(doc_table, first_pos, half_rows, 0)
    return (places, owners)


def joined_meta(first, second):
    return (jnp.concatenate((first[0], second[0]), 0), jnp.concatenate((first[1], second[1]), 0))


def visible(query_meta, key_meta):
    return (key_meta[0][None, :] <= query_meta[0][:, None]) & (
        key_meta[1][None, :] == query_meta[1][:, None]
    )


def tile_scores(query_tile, key_rows, scaling):
    return (
        jnp.einsum("tkgd,skd->kgts", query_tile, key_rows, preferred_element_type=jnp.float32)
        * scaling
    )


def forward_tile(carried, masked, query_tile, key_tile, value_tile, scaling):
    peak_score, totals, summed = carried
    kv_local = query_tile.shape[1]
    key_rows = key_tile.reshape(key_tile.shape[0], kv_local, -1)
    value_rows = value_tile.reshape(value_tile.shape[0], kv_local, -1)
    scores = jnp.where(masked, tile_scores(query_tile, key_rows, scaling), NEGATIVE)
    new_peak = jnp.maximum(peak_score, jnp.max(scores, axis=-1))
    weights = jnp.where(masked, jnp.exp(scores - new_peak[..., None]), 0.0)
    factor = jnp.exp(peak_score - new_peak)
    summed = summed * factor[..., None] + jnp.einsum(
        "kgts,skd->kgtd",
        weights.astype(jnp.bfloat16),
        value_rows,
        preferred_element_type=jnp.float32,
    )
    return (new_peak, totals * factor + jnp.sum(weights, axis=-1), summed)


def backward_tile(
    carried, masked, query_tile, grad_tile, lse_tile, delta_tile, key_tile, value_tile, scaling
):
    grad_query, grad_key, grad_value = carried
    kv_local = query_tile.shape[1]
    key_rows = key_tile.reshape(key_tile.shape[0], kv_local, -1)
    value_rows = value_tile.reshape(value_tile.shape[0], kv_local, -1)
    scores = tile_scores(query_tile, key_rows, scaling)
    prob_tile = jnp.where(masked, jnp.exp(scores - lse_tile[..., None]), 0.0)
    grad_value = grad_value + jnp.einsum(
        "kgts,tkgd->skd",
        prob_tile.astype(jnp.bfloat16),
        grad_tile,
        preferred_element_type=jnp.float32,
    )
    dot_tile = jnp.einsum(
        "tkgd,skd->kgts", grad_tile, value_rows, preferred_element_type=jnp.float32
    )
    slopes = (prob_tile * (dot_tile - delta_tile[..., None])).astype(jnp.bfloat16)
    grad_query = grad_query + jnp.einsum(
        "kgts,skd->tkgd", slopes, key_rows, preferred_element_type=jnp.float32
    )
    grad_key = grad_key + jnp.einsum(
        "kgts,tkgd->skd", slopes, query_tile, preferred_element_type=jnp.float32
    )
    return (grad_query, grad_key, grad_value)


def anchors(member, cycle_size, counter):
    return ((member - counter) % cycle_size, (member - counter) % cycle_size)


def advance(current):
    return tuple(passed_along((current[0], current[1], current[2], current[3]), "outer", 1))


def rotate_grads(key_acc, value_acc):
    moved = (
        passed_along(key_acc.astype(jnp.bfloat16), "outer", 1).astype(key_acc.dtype),
        passed_along(value_acc.astype(jnp.bfloat16), "outer", 1).astype(value_acc.dtype),
    )
    return (moved[0], moved[1])


def on_device(
    queries, keys, values, grad_out, hidden_in, adapter_a, adapter_b, block_order, doc_ids
):
    cycle_size = lax.axis_size("outer")
    member = lax.axis_index("outer")
    tokens = queries.shape[0]
    half_rows = tokens // 2
    kv_local = keys.shape[1] // HEAD_DIM
    grp_local = queries.shape[1] // (kv_local * HEAD_DIM)
    scaling = HEAD_DIM ** (-0.5)
    query_rows = queries.reshape(tokens, kv_local, grp_local, HEAD_DIM)
    grad_rows = grad_out.reshape(tokens, kv_local, grp_local, HEAD_DIM)
    own_meta = joined_meta(
        block_meta(block_order, doc_ids, 2 * member, half_rows),
        block_meta(block_order, doc_ids, 2 * member + 1, half_rows),
    )
    local_keys = (keys[:half_rows], values[:half_rows], keys[half_rows:], values[half_rows:])
    low_partial = jnp.dot(hidden_in, adapter_a, preferred_element_type=jnp.float32)
    low_rank = lax.psum(low_partial, ("head", "inner")).astype(jnp.bfloat16)

    def sweep(counter, current, handle, carried):
        upper_src, lower_src = anchors(member, cycle_size, counter)
        key_meta = joined_meta(
            block_meta(block_order, doc_ids, 2 * upper_src, half_rows),
            block_meta(block_order, doc_ids, 2 * lower_src + 1, half_rows),
        )
        masked = visible(own_meta, key_meta)
        key_tile = jnp.concatenate((current[0], current[2]), 0)
        value_tile = jnp.concatenate((current[1], current[3]), 0)

        def active(present):
            return handle(present, masked, key_tile, value_tile)

        def resting(present):
            return present

        return lax.cond(jnp.any(masked), active, resting, carried)

    def forward_handle(present, masked, key_tile, value_tile):
        return forward_tile(present, masked, query_rows, key_tile, value_tile, scaling)

    start_state = (
        jnp.full((kv_local, grp_local, tokens), NEGATIVE, jnp.float32),
        jnp.zeros((kv_local, grp_local, tokens), jnp.float32),
        jnp.zeros((kv_local, grp_local, tokens, HEAD_DIM), jnp.float32),
    )

    def forward_turn(counter, loop_state):
        current, state = loop_state
        state = sweep(counter, current, forward_handle, state)
        return (advance(current), state)

    current, state = lax.fori_loop(0, cycle_size - 1, forward_turn, (local_keys, start_state))
    state = sweep(cycle_size - 1, current, forward_handle, state)
    peak_score, totals, summed = state
    lse_rows = peak_score + jnp.log(totals)
    output = summed / totals[..., None]
    delta_rows = jnp.sum(
        output * jnp.transpose(grad_rows, (1, 2, 0, 3)).astype(jnp.float32), axis=-1
    )
    empty_query = jnp.zeros((tokens, kv_local, grp_local, HEAD_DIM), jnp.float32)

    def backward_handle(present, masked, key_tile, value_tile):
        return backward_tile(
            present,
            masked,
            query_rows,
            grad_rows,
            lse_rows,
            delta_rows,
            key_tile,
            value_tile,
            scaling,
        )

    def backward_turn(counter, loop_state):
        current, carried = loop_state
        grad_query, key_acc, value_acc = sweep(counter, current, backward_handle, carried)
        key_acc, value_acc = rotate_grads(key_acc, value_acc)
        return (advance(current), (grad_query, key_acc, value_acc))

    empty_keys = jnp.zeros((tokens, kv_local, HEAD_DIM), jnp.float32)
    current, carried = lax.fori_loop(
        0, cycle_size - 1, backward_turn, (local_keys, (empty_query, empty_keys, empty_keys))
    )
    grad_queries, key_acc, value_acc = sweep(cycle_size - 1, current, backward_handle, carried)
    key_acc, value_acc = rotate_grads(key_acc, value_acc)
    key_acc, value_acc = (
        lax.psum(key_acc.astype(jnp.bfloat16), "inner").astype(jnp.float32),
        lax.psum(value_acc.astype(jnp.bfloat16), "inner").astype(jnp.float32),
    )
    grad_query = (grad_queries * scaling).astype(jnp.bfloat16).reshape(tokens, -1)
    grad_key = (key_acc * scaling).astype(jnp.bfloat16).reshape(tokens, -1)
    grad_value = value_acc.astype(jnp.bfloat16).reshape(tokens, -1)
    back_partial = lax.dot_general(
        grad_key, adapter_b, (((1,), (1,)), ((), ())), preferred_element_type=jnp.float32
    )
    back_rank = lax.psum(back_partial, "head").astype(jnp.bfloat16)
    grad_a_part = lax.dot_general(
        hidden_in, back_rank, (((0,), (0,)), ((), ())), preferred_element_type=jnp.float32
    )
    grad_b_part = lax.dot_general(
        low_rank, grad_key, (((0,), (0,)), ((), ())), preferred_element_type=jnp.float32
    )
    grad_a, grad_b = lax.psum((grad_a_part, grad_b_part), "outer")
    return (grad_query, grad_key, grad_value, grad_a, grad_b)


def solution(mesh):
    in_specs = (
        P("outer", ("head", "inner")),
        P("outer", "head"),
        P("outer", "head"),
        P("outer", ("head", "inner")),
        P("outer", ("head", "inner")),
        P(("head", "inner"), None),
        P(None, "head"),
        P(),
        P(),
    )
    out_specs = (
        P("outer", ("head", "inner")),
        P("outer", "head"),
        P("outer", "head"),
        P(("head", "inner"), None),
        P(None, "head"),
    )
    return jax.shard_map(
        on_device, mesh=mesh, in_specs=in_specs, out_specs=out_specs, check_vma=False
    )
```

profile of v0, /device:TPU:0, one launch (start us, length us, event | category | flops | bytes accessed | tf_op | source)
XLA Modules:
  0.0 191.0 jit_solution(2732203361276319303)
XLA Ops:
  14.9 30.7 %while.55 = (s32[]{:T(128)}, bf16[128,128]{1,0:T(8,128)(2,1)S(1)}, bf16[128,128]{1,0:T(8,128)(2,1)S(1)}, bf16[128,128]{1,0:T(8,128)(2,1)S(1)}, bf16[128,128]{1,0...) while((s32[]{:T(128)}, bf16[128,128]{1,0:T(8,128)(2,1)S(1)}, ...), condition=%wide.region_7.8_spmd, body=%wide.region_1.7_spmd.sunk | while | flops 68946208 | bytes 3714876 | solution.py:156
  14.9 3.1 %collective-permute-start = (bf16[128,128]{1,0:T(8,128)(2,1)S(1)}, bf16[128,128]{1,0:T(8,128)(2,1)S(1)}, u32[]{:S(2)}, u32[]{:S(2)}) collective-permute-start(bf16[128,128]{1,0:T(8,128)(2,1)S(1)} %copy.63), channel_id=1, source_target_pairs={{0,4},{4,8},{8,12},{12,0},{1,5},{5,9},{9,13},{13,1},{2,6},{6,10},{... | collective-permute-start | bytes 98312 | tf_op jit(solution)/shard_map/while/body/eval_jaxpr/ppermute | solution.py:15
  18.1 1.6 collective-permute-start.1
  19.6 1.6 collective-permute-start.2
  23.3 0.8 fusion.112
  24.7 0.8 conditional.9
  25.6 1.3 collective-permute-done.3
  27.4 1.6 collective-permute-start.1
  29.0 1.6 collective-permute-start.2
  30.6 1.3 collective-permute-start.3
  33.9 0.8 fusion.112
  35.3 0.8 conditional.9
  36.8 1.6 collective-permute-start.1
  38.4 0.8 collective-permute-start.2
  39.1 2.1 %collective-permute-start.3 = (bf16[128,128]{1,0:T(8,128)(2,1)S(1)}, bf16[128,128]{1,0:T(8,128)(2,1)S(1)}, u32[]{:S(2)}, u32[]{:S(2)}) collective-permute-start(bf16[128,128]{1,0:T(8,128)(2,1)S(1)} %copy.66), channel_id=1, source_target_pairs={{0,4},{4,8},{8,12},{12,0},{1,5},{5,9},{9,13},{13,1},{2,6},{6,10},{... | collective-permute-start | bytes 98312 | tf_op jit(solution)/shard_map/while/body/eval_jaxpr/ppermute | solution.py:15
  43.3 0.8 fusion.112
  44.7 0.8 conditional.9
  45.6 0.9 conditional.4
  46.7 50.4 %while.56 = (s32[]{:T(128)}, bf16[128,128]{1,0:T(8,128)(2,1)S(1)}, bf16[128,128]{1,0:T(8,128)(2,1)S(1)}, bf16[128,128]{1,0:T(8,128)(2,1)S(1)}, bf16[128,128]{1,0...) while((s32[]{:T(128)}, bf16[128,128]{1,0:T(8,128)(2,1)S(1)}, ...), condition=%wide.region_17.18_spmd.clone, body=%wide.region_13.0_spmd.clone.sunk | while | flops 169542432 | bytes 7159750 | solution.py:186
  48.8 0.8 fusion.115
  50.3 1.3 conditional.10
  52.1 1.6 collective-permute-start.8
  53.8 2.8 %collective-permute-start.5 = (bf16[128,128]{1,0:T(8,128)(2,1)S(1)}, bf16[128,128]{1,0:T(8,128)(2,1)S(1)}, u32[]{:S(2)}, u32[]{:S(2)}) collective-permute-start(bf16[128,128]{1,0:T(8,128)(2,1)S(1)} %copy.96), channel_id=1, source_target_pairs={{0,4},{4,8},{8,12},{12,0},{1,5},{5,9},{9,13},{13,1},{2,6},{6,10},{... | collective-permute-start | bytes 98312 | tf_op jit(solution)/shard_map/while/body/eval_jaxpr/ppermute | solution.py:15
  57.1 0.9 collective-permute-done.9
  59.8 2.5 %collective-permute-done.6 = bf16[128,128]{1,0:T(8,128)(2,1)S(1)} collective-permute-done((bf16[128,128]{1,0:T(8,128)(2,1)S(1)}, bf16[128,128]{1,0:T(8,128)(2,1)S(1)}, u32[]{:S(2)}, u32[]{:S(2)}) %collective-permute-start.6) | collective-permute-done | bytes 32800 | tf_op jit(solution)/shard_map/while/body/eval_jaxpr/ppermute | solution.py:15
  62.3 1.4 collective-permute-done.7
  65.8 0.8 fusion.115
  67.3 1.3 conditional.10
  69.4 4.3 %collective-permute-start.5 = (bf16[128,128]{1,0:T(8,128)(2,1)S(1)}, bf16[128,128]{1,0:T(8,128)(2,1)S(1)}, u32[]{:S(2)}, u32[]{:S(2)}) collective-permute-start(bf16[128,128]{1,0:T(8,128)(2,1)S(1)} %copy.96), channel_id=1, source_target_pairs={{0,4},{4,8},{8,12},{12,0},{1,5},{5,9},{9,13},{13,1},{2,6},{6,10},{... | collective-permute-start | bytes 98312 | tf_op jit(solution)/shard_map/while/body/eval_jaxpr/ppermute | solution.py:15
  73.7 1.0 collective-permute-done.9
  76.1 3.3 %collective-permute-done.6 = bf16[128,128]{1,0:T(8,128)(2,1)S(1)} collective-permute-done((bf16[128,128]{1,0:T(8,128)(2,1)S(1)}, bf16[128,128]{1,0:T(8,128)(2,1)S(1)}, u32[]{:S(2)}, u32[]{:S(2)}) %collective-permute-start.6) | collective-permute-done | bytes 32800 | tf_op jit(solution)/shard_map/while/body/eval_jaxpr/ppermute | solution.py:15
  79.4 1.0 collective-permute-done.7
  82.5 0.8 fusion.115
  84.0 1.3 conditional.10
  85.4 0.8 collective-permute-start.4
  86.2 4.1 %collective-permute-start.5 = (bf16[128,128]{1,0:T(8,128)(2,1)S(1)}, bf16[128,128]{1,0:T(8,128)(2,1)S(1)}, u32[]{:S(2)}, u32[]{:S(2)}) collective-permute-start(bf16[128,128]{1,0:T(8,128)(2,1)S(1)} %copy.96), channel_id=1, source_target_pairs={{0,4},{4,8},{8,12},{12,0},{1,5},{5,9},{9,13},{13,1},{2,6},{6,10},{... | collective-permute-start | bytes 98312 | tf_op jit(solution)/shard_map/while/body/eval_jaxpr/ppermute | solution.py:15
  90.4 1.0 collective-permute-done.9
  93.2 2.8 %collective-permute-done.6 = bf16[128,128]{1,0:T(8,128)(2,1)S(1)} collective-permute-done((bf16[128,128]{1,0:T(8,128)(2,1)S(1)}, bf16[128,128]{1,0:T(8,128)(2,1)S(1)}, u32[]{:S(2)}, u32[]{:S(2)}) %collective-permute-start.6) | collective-permute-done | bytes 32800 | tf_op jit(solution)/shard_map/while/body/eval_jaxpr/ppermute | solution.py:15
  96.0 1.0 collective-permute-done.7
  97.1 1.3 conditional.5
  99.5 5.0 %collective-permute-done.11 = bf16[256,1,128]{2,0,1:T(8,128)(2,1)S(1)} collective-permute-done((bf16[256,1,128]{2,0,1:T(8,128)(2,1)S(1)}, bf16[256,1,128]{2,0,1:T(8,128)(2,1)S(1)}, u32[]{:S(2)}, u32[]{:S(2)}) %collective-permute-start.11) | collective-permute-done | bytes 65568 | tf_op jit(solution)/shard_map/ppermute | solution.py:15
  106.7 23.6 %psum.46 = bf16[256,16]{1,0:T(8,128)(2,1)S(1)} all-reduce(f32[256,16]{1,0:T(8,128)S(1)} %fusion.90), channel_id=1, replica_groups=mesh['head'=2,'outer'=4,'inner'=4] {'head','inner'}, use_global_device_ids=true, to_apply=%region_24.25 | all-reduce | flops 4096 | bytes 24576 | tf_op jit(solution)/shard_map/psum | solution.py:122
  130.3 6.6 %all-reduce.6.cloned.1.call-done = (bf16[256,1,128]{2,0,1:T(8,128)(2,1)}, bf16[256,128]{1,0:T(8,128)(2,1)}) async-done(((bf16[256,1,128]{2,0,1:T(8,128)(2,1)}, bf16[256,128]{1,0:T(8,128)(2,1)}), (bf16[256,1,128]{2,0,1:T(8,128)(2,1)}, bf16[256,128]{1,0:T(8,128)(2,1)})) %all-reduce.6.cloned.1.call-update) | async-done | bytes 131088 | tf_op jit(solution)/shard_map/psum | solution.py:192
  136.9 0.9 fusion.71
  138.0 9.9 %psum.44 = bf16[256,16]{1,0:T(8,128)(2,1)S(1)} all-reduce(f32[256,16]{1,0:T(8,128)S(1)} %fusion.89), channel_id=1, replica_groups=mesh['head'=2,'outer'=4,'inner'=4] {'head'}, use_global_device_ids=true, to_apply=%region_22.23 | all-reduce | flops 4096 | bytes 24576 | tf_op jit(solution)/shard_map/psum | solution.py:201
  147.8 0.8 convolution_bitcast_fusion.10
  148.9 12.7 %psum.47 = f32[16,128]{1,0:T(8,128)} all-reduce(f32[16,128]{1,0:T(8,128)S(1)} %fusion.91), channel_id=1, replica_groups=mesh['head'=2,'outer'=4,'inner'=4] {'outer'}, use_global_device_ids=true, to_apply=%region_25.26 | all-reduce | flops 2048 | bytes 16384 | tf_op jit(solution)/shard_map/psum | solution.py:208
  161.6 21.1 %all-reduce.4.cloned.1.call-done = f32[1024,16]{0,1:T(8,128)} async-done(((f32[1024,16]{0,1:T(8,128)}), f32[1024,16]{0,1:T(8,128)}) %all-reduce.4.cloned.1.call-update) | async-done | bytes 65552 | tf_op jit(solution)/shard_map/psum | solution.py:208
  (230 shorter events, 30.2 us)
Async XLA Ops:
  7.2 91.4 %copy-start = (bf16[256,1024]{1,0:T(8,128)(2,1)S(1)}, bf16[256,1024]{1,0:T(8,128)(2,1)}, u32[]{:S(2)}) copy-start(bf16[256,1024]{1,0:T(8,128)(2,1)} %param.25) | copy-start | bytes 1572868
  7.2 129.8 %all-reduce.6.cloned.1.call-start = ((), (), s32[]{:S(2)}) async-start(), calls=%async_computation.1 | async-start | bytes 262144 | tf_op jit(solution)/shard_map/psum | solution.py:192
  7.3 4.0 %copy-start.11 = (s32[1024]{0:T(1024)S(1)}, s32[1024]{0:T(1024)}, u32[]{:S(2)}) copy-start(s32[1024]{0:T(1024)} %param.29) | copy-start | bytes 12292
  7.3 0.7 copy-start.2
  7.3 5.5 %copy-start.3 = (bf16[256,256]{1,0:T(8,128)(2,1)S(1)}, bf16[256,256]{1,0:T(8,128)(2,1)}, u32[]{:S(2)}) copy-start(bf16[256,256]{1,0:T(8,128)(2,1)} %param.21) | copy-start | bytes 393220
  12.9 0.9 copy-start.4
  13.9 0.8 copy-start.9
  13.9 0.9 copy-start.10
  14.9 10.6 %collective-permute-start = (bf16[128,128]{1,0:T(8,128)(2,1)S(1)}, bf16[128,128]{1,0:T(8,128)(2,1)S(1)}, u32[]{:S(2)}, u32[]{:S(2)}) collective-permute-start(bf16[128,128]{1,0:T(8,128)(2,1)S(1)} %copy.63), channel_id=1, source_target_pairs={{0,4},{4,8},{8,12},{12,0},{1,5},{5,9},{9,13},{13,1},{2,6},{6,10},{... | collective-permute-start | bytes 98312 | tf_op jit(solution)/shard_map/while/body/eval_jaxpr/ppermute | solution.py:15
  18.1 7.5 %collective-permute-start.1 = (bf16[128,128]{1,0:T(8,128)(2,1)S(1)}, bf16[128,128]{1,0:T(8,128)(2,1)S(1)}, u32[]{:S(2)}, u32[]{:S(2)}) collective-permute-start(bf16[128,128]{1,0:T(8,128)(2,1)S(1)} %copy.64), channel_id=1, source_target_pairs={{0,4},{4,8},{8,12},{12,0},{1,5},{5,9},{9,13},{13,1},{2,6},{6,10},{... | collective-permute-start | bytes 98312 | tf_op jit(solution)/shard_map/while/body/eval_jaxpr/ppermute | solution.py:15
  19.6 6.0 %collective-permute-start.2 = (bf16[128,128]{1,0:T(8,128)(2,1)S(1)}, bf16[128,128]{1,0:T(8,128)(2,1)S(1)}, u32[]{:S(2)}, u32[]{:S(2)}) collective-permute-start(bf16[128,128]{1,0:T(8,128)(2,1)S(1)} %copy.65), channel_id=1, source_target_pairs={{0,4},{4,8},{8,12},{12,0},{1,5},{5,9},{9,13},{13,1},{2,6},{6,10},{... | collective-permute-start | bytes 98312 | tf_op jit(solution)/shard_map/while/body/eval_jaxpr/ppermute | solution.py:15
  21.2 5.7 %collective-permute-start.3 = (bf16[128,128]{1,0:T(8,128)(2,1)S(1)}, bf16[128,128]{1,0:T(8,128)(2,1)S(1)}, u32[]{:S(2)}, u32[]{:S(2)}) collective-permute-start(bf16[128,128]{1,0:T(8,128)(2,1)S(1)} %copy.66), channel_id=1, source_target_pairs={{0,4},{4,8},{8,12},{12,0},{1,5},{5,9},{9,13},{13,1},{2,6},{6,10},{... | collective-permute-start | bytes 98312 | tf_op jit(solution)/shard_map/while/body/eval_jaxpr/ppermute | solution.py:15
  26.9 9.2 %collective-permute-start = (bf16[128,128]{1,0:T(8,128)(2,1)S(1)}, bf16[128,128]{1,0:T(8,128)(2,1)S(1)}, u32[]{:S(2)}, u32[]{:S(2)}) collective-permute-start(bf16[128,128]{1,0:T(8,128)(2,1)S(1)} %copy.63), channel_id=1, source_target_pairs={{0,4},{4,8},{8,12},{12,0},{1,5},{5,9},{9,13},{13,1},{2,6},{6,10},{... | collective-permute-start | bytes 98312 | tf_op jit(solution)/shard_map/while/body/eval_jaxpr/ppermute | solution.py:15
  27.4 8.8 %collective-permute-start.1 = (bf16[128,128]{1,0:T(8,128)(2,1)S(1)}, bf16[128,128]{1,0:T(8,128)(2,1)S(1)}, u32[]{:S(2)}, u32[]{:S(2)}) collective-permute-start(bf16[128,128]{1,0:T(8,128)(2,1)S(1)} %copy.64), channel_id=1, source_target_pairs={{0,4},{4,8},{8,12},{12,0},{1,5},{5,9},{9,13},{13,1},{2,6},{6,10},{... | collective-permute-start | bytes 98312 | tf_op jit(solution)/shard_map/while/body/eval_jaxpr/ppermute | solution.py:15
  29.0 7.2 %collective-permute-start.2 = (bf16[128,128]{1,0:T(8,128)(2,1)S(1)}, bf16[128,128]{1,0:T(8,128)(2,1)S(1)}, u32[]{:S(2)}, u32[]{:S(2)}) collective-permute-start(bf16[128,128]{1,0:T(8,128)(2,1)S(1)} %copy.65), channel_id=1, source_target_pairs={{0,4},{4,8},{8,12},{12,0},{1,5},{5,9},{9,13},{13,1},{2,6},{6,10},{... | collective-permute-start | bytes 98312 | tf_op jit(solution)/shard_map/while/body/eval_jaxpr/ppermute | solution.py:15
  30.6 5.7 %collective-permute-start.3 = (bf16[128,128]{1,0:T(8,128)(2,1)S(1)}, bf16[128,128]{1,0:T(8,128)(2,1)S(1)}, u32[]{:S(2)}, u32[]{:S(2)}) collective-permute-start(bf16[128,128]{1,0:T(8,128)(2,1)S(1)} %copy.66), channel_id=1, source_target_pairs={{0,4},{4,8},{8,12},{12,0},{1,5},{5,9},{9,13},{13,1},{2,6},{6,10},{... | collective-permute-start | bytes 98312 | tf_op jit(solution)/shard_map/while/body/eval_jaxpr/ppermute | solution.py:15
  36.3 9.2 %collective-permute-start = (bf16[128,128]{1,0:T(8,128)(2,1)S(1)}, bf16[128,128]{1,0:T(8,128)(2,1)S(1)}, u32[]{:S(2)}, u32[]{:S(2)}) collective-permute-start(bf16[128,128]{1,0:T(8,128)(2,1)S(1)} %copy.63), channel_id=1, source_target_pairs={{0,4},{4,8},{8,12},{12,0},{1,5},{5,9},{9,13},{13,1},{2,6},{6,10},{... | collective-permute-start | bytes 98312 | tf_op jit(solution)/shard_map/while/body/eval_jaxpr/ppermute | solution.py:15
  36.8 8.8 %collective-permute-start.1 = (bf16[128,128]{1,0:T(8,128)(2,1)S(1)}, bf16[128,128]{1,0:T(8,128)(2,1)S(1)}, u32[]{:S(2)}, u32[]{:S(2)}) collective-permute-start(bf16[128,128]{1,0:T(8,128)(2,1)S(1)} %copy.64), channel_id=1, source_target_pairs={{0,4},{4,8},{8,12},{12,0},{1,5},{5,9},{9,13},{13,1},{2,6},{6,10},{... | collective-permute-start | bytes 98312 | tf_op jit(solution)/shard_map/while/body/eval_jaxpr/ppermute | solution.py:15
  38.4 7.2 %collective-permute-start.2 = (bf16[128,128]{1,0:T(8,128)(2,1)S(1)}, bf16[128,128]{1,0:T(8,128)(2,1)S(1)}, u32[]{:S(2)}, u32[]{:S(2)}) collective-permute-start(bf16[128,128]{1,0:T(8,128)(2,1)S(1)} %copy.65), channel_id=1, source_target_pairs={{0,4},{4,8},{8,12},{12,0},{1,5},{5,9},{9,13},{13,1},{2,6},{6,10},{... | collective-permute-start | bytes 98312 | tf_op jit(solution)/shard_map/while/body/eval_jaxpr/ppermute | solution.py:15
  39.1 6.4 %collective-permute-start.3 = (bf16[128,128]{1,0:T(8,128)(2,1)S(1)}, bf16[128,128]{1,0:T(8,128)(2,1)S(1)}, u32[]{:S(2)}, u32[]{:S(2)}) collective-permute-start(bf16[128,128]{1,0:T(8,128)(2,1)S(1)} %copy.66), channel_id=1, source_target_pairs={{0,4},{4,8},{8,12},{12,0},{1,5},{5,9},{9,13},{13,1},{2,6},{6,10},{... | collective-permute-start | bytes 98312 | tf_op jit(solution)/shard_map/while/body/eval_jaxpr/ppermute | solution.py:15
  51.6 6.5 %collective-permute-start.9 = (bf16[256,1,128]{2,0,1:T(8,128)(2,1)S(1)}, bf16[256,1,128]{2,0,1:T(8,128)(2,1)S(1)}, u32[]{:S(2)}, u32[]{:S(2)}) collective-permute-start(bf16[256,1,128]{2,0,1:T(8,128)(2,1)S(1)} %convert_element_type.175), channel_id=1, source_target_pairs={{0,4},{4,8},{8,12},{12,0},{1,5},{5,9},{9,13},{13,1},{2,6},{6,10},{... | collective-permute-start | bytes 196616 | tf_op jit(solution)/shard_map/while/body/eval_jaxpr/ppermute | solution.py:15
  52.1 6.6 %collective-permute-start.8 = (bf16[256,1,128]{2,0,1:T(8,128)(2,1)S(1)}, bf16[256,1,128]{2,0,1:T(8,128)(2,1)S(1)}, u32[]{:S(2)}, u32[]{:S(2)}) collective-permute-start(bf16[256,1,128]{2,0,1:T(8,128)(2,1)S(1)} %convert_element_type.173), channel_id=1, source_target_pairs={{0,4},{4,8},{8,12},{12,0},{1,5},{5,9},{9,13},{13,1},{2,6},{6,10},{... | collective-permute-start | bytes 196616 | tf_op jit(solution)/shard_map/while/body/eval_jaxpr/ppermute | solution.py:15
  53.7 5.7 %collective-permute-start.4 = (bf16[128,128]{1,0:T(8,128)(2,1)S(1)}, bf16[128,128]{1,0:T(8,128)(2,1)S(1)}, u32[]{:S(2)}, u32[]{:S(2)}) collective-permute-start(bf16[128,128]{1,0:T(8,128)(2,1)S(1)} %copy.95), channel_id=1, source_target_pairs={{0,4},{4,8},{8,12},{12,0},{1,5},{5,9},{9,13},{13,1},{2,6},{6,10},{... | collective-permute-start | bytes 98312 | tf_op jit(solution)/shard_map/while/body/eval_jaxpr/ppermute | solution.py:15
  53.8 6.0 %collective-permute-start.5 = (bf16[128,128]{1,0:T(8,128)(2,1)S(1)}, bf16[128,128]{1,0:T(8,128)(2,1)S(1)}, u32[]{:S(2)}, u32[]{:S(2)}) collective-permute-start(bf16[128,128]{1,0:T(8,128)(2,1)S(1)} %copy.96), channel_id=1, source_target_pairs={{0,4},{4,8},{8,12},{12,0},{1,5},{5,9},{9,13},{13,1},{2,6},{6,10},{... | collective-permute-start | bytes 98312 | tf_op jit(solution)/shard_map/while/body/eval_jaxpr/ppermute | solution.py:15
  56.6 5.7 %collective-permute-start.6 = (bf16[128,128]{1,0:T(8,128)(2,1)S(1)}, bf16[128,128]{1,0:T(8,128)(2,1)S(1)}, u32[]{:S(2)}, u32[]{:S(2)}) collective-permute-start(bf16[128,128]{1,0:T(8,128)(2,1)S(1)} %copy.97), channel_id=1, source_target_pairs={{0,4},{4,8},{8,12},{12,0},{1,5},{5,9},{9,13},{13,1},{2,6},{6,10},{... | collective-permute-start | bytes 98312 | tf_op jit(solution)/shard_map/while/body/eval_jaxpr/ppermute | solution.py:15
  58.0 5.7 %collective-permute-start.7 = (bf16[128,128]{1,0:T(8,128)(2,1)S(1)}, bf16[128,128]{1,0:T(8,128)(2,1)S(1)}, u32[]{:S(2)}, u32[]{:S(2)}) collective-permute-start(bf16[128,128]{1,0:T(8,128)(2,1)S(1)} %copy.98), channel_id=1, source_target_pairs={{0,4},{4,8},{8,12},{12,0},{1,5},{5,9},{9,13},{13,1},{2,6},{6,10},{... | collective-permute-start | bytes 98312 | tf_op jit(solution)/shard_map/while/body/eval_jaxpr/ppermute | solution.py:15
  68.6 6.1 %collective-permute-start.9 = (bf16[256,1,128]{2,0,1:T(8,128)(2,1)S(1)}, bf16[256,1,128]{2,0,1:T(8,128)(2,1)S(1)}, u32[]{:S(2)}, u32[]{:S(2)}) collective-permute-start(bf16[256,1,128]{2,0,1:T(8,128)(2,1)S(1)} %convert_element_type.175), channel_id=1, source_target_pairs={{0,4},{4,8},{8,12},{12,0},{1,5},{5,9},{9,13},{13,1},{2,6},{6,10},{... | collective-permute-start | bytes 196616 | tf_op jit(solution)/shard_map/while/body/eval_jaxpr/ppermute | solution.py:15
  68.7 6.7 %collective-permute-start.8 = (bf16[256,1,128]{2,0,1:T(8,128)(2,1)S(1)}, bf16[256,1,128]{2,0,1:T(8,128)(2,1)S(1)}, u32[]{:S(2)}, u32[]{:S(2)}) collective-permute-start(bf16[256,1,128]{2,0,1:T(8,128)(2,1)S(1)} %convert_element_type.173), channel_id=1, source_target_pairs={{0,4},{4,8},{8,12},{12,0},{1,5},{5,9},{9,13},{13,1},{2,6},{6,10},{... | collective-permute-start | bytes 196616 | tf_op jit(solution)/shard_map/while/body/eval_jaxpr/ppermute | solution.py:15
  68.7 7.0 %collective-permute-start.4 = (bf16[128,128]{1,0:T(8,128)(2,1)S(1)}, bf16[128,128]{1,0:T(8,128)(2,1)S(1)}, u32[]{:S(2)}, u32[]{:S(2)}) collective-permute-start(bf16[128,128]{1,0:T(8,128)(2,1)S(1)} %copy.95), channel_id=1, source_target_pairs={{0,4},{4,8},{8,12},{12,0},{1,5},{5,9},{9,13},{13,1},{2,6},{6,10},{... | collective-permute-start | bytes 98312 | tf_op jit(solution)/shard_map/while/body/eval_jaxpr/ppermute | solution.py:15
  69.4 6.7 %collective-permute-start.5 = (bf16[128,128]{1,0:T(8,128)(2,1)S(1)}, bf16[128,128]{1,0:T(8,128)(2,1)S(1)}, u32[]{:S(2)}, u32[]{:S(2)}) collective-permute-start(bf16[128,128]{1,0:T(8,128)(2,1)S(1)} %copy.96), channel_id=1, source_target_pairs={{0,4},{4,8},{8,12},{12,0},{1,5},{5,9},{9,13},{13,1},{2,6},{6,10},{... | collective-permute-start | bytes 98312 | tf_op jit(solution)/shard_map/while/body/eval_jaxpr/ppermute | solution.py:15
  73.7 5.7 %collective-permute-start.6 = (bf16[128,128]{1,0:T(8,128)(2,1)S(1)}, bf16[128,128]{1,0:T(8,128)(2,1)S(1)}, u32[]{:S(2)}, u32[]{:S(2)}) collective-permute-start(bf16[128,128]{1,0:T(8,128)(2,1)S(1)} %copy.97), channel_id=1, source_target_pairs={{0,4},{4,8},{8,12},{12,0},{1,5},{5,9},{9,13},{13,1},{2,6},{6,10},{... | collective-permute-start | bytes 98312 | tf_op jit(solution)/shard_map/while/body/eval_jaxpr/ppermute | solution.py:15
  74.7 5.7 %collective-permute-start.7 = (bf16[128,128]{1,0:T(8,128)(2,1)S(1)}, bf16[128,128]{1,0:T(8,128)(2,1)S(1)}, u32[]{:S(2)}, u32[]{:S(2)}) collective-permute-start(bf16[128,128]{1,0:T(8,128)(2,1)S(1)} %copy.98), channel_id=1, source_target_pairs={{0,4},{4,8},{8,12},{12,0},{1,5},{5,9},{9,13},{13,1},{2,6},{6,10},{... | collective-permute-start | bytes 98312 | tf_op jit(solution)/shard_map/while/body/eval_jaxpr/ppermute | solution.py:15
  85.2 6.1 %collective-permute-start.9 = (bf16[256,1,128]{2,0,1:T(8,128)(2,1)S(1)}, bf16[256,1,128]{2,0,1:T(8,128)(2,1)S(1)}, u32[]{:S(2)}, u32[]{:S(2)}) collective-permute-start(bf16[256,1,128]{2,0,1:T(8,128)(2,1)S(1)} %convert_element_type.175), channel_id=1, source_target_pairs={{0,4},{4,8},{8,12},{12,0},{1,5},{5,9},{9,13},{13,1},{2,6},{6,10},{... | collective-permute-start | bytes 196616 | tf_op jit(solution)/shard_map/while/body/eval_jaxpr/ppermute | solution.py:15
  85.3 6.7 %collective-permute-start.8 = (bf16[256,1,128]{2,0,1:T(8,128)(2,1)S(1)}, bf16[256,1,128]{2,0,1:T(8,128)(2,1)S(1)}, u32[]{:S(2)}, u32[]{:S(2)}) collective-permute-start(bf16[256,1,128]{2,0,1:T(8,128)(2,1)S(1)} %convert_element_type.173), channel_id=1, source_target_pairs={{0,4},{4,8},{8,12},{12,0},{1,5},{5,9},{9,13},{13,1},{2,6},{6,10},{... | collective-permute-start | bytes 196616 | tf_op jit(solution)/shard_map/while/body/eval_jaxpr/ppermute | solution.py:15
  85.4 7.1 %collective-permute-start.4 = (bf16[128,128]{1,0:T(8,128)(2,1)S(1)}, bf16[128,128]{1,0:T(8,128)(2,1)S(1)}, u32[]{:S(2)}, u32[]{:S(2)}) collective-permute-start(bf16[128,128]{1,0:T(8,128)(2,1)S(1)} %copy.95), channel_id=1, source_target_pairs={{0,4},{4,8},{8,12},{12,0},{1,5},{5,9},{9,13},{13,1},{2,6},{6,10},{... | collective-permute-start | bytes 98312 | tf_op jit(solution)/shard_map/while/body/eval_jaxpr/ppermute | solution.py:15
  86.2 7.0 %collective-permute-start.5 = (bf16[128,128]{1,0:T(8,128)(2,1)S(1)}, bf16[128,128]{1,0:T(8,128)(2,1)S(1)}, u32[]{:S(2)}, u32[]{:S(2)}) collective-permute-start(bf16[128,128]{1,0:T(8,128)(2,1)S(1)} %copy.96), channel_id=1, source_target_pairs={{0,4},{4,8},{8,12},{12,0},{1,5},{5,9},{9,13},{13,1},{2,6},{6,10},{... | collective-permute-start | bytes 98312 | tf_op jit(solution)/shard_map/while/body/eval_jaxpr/ppermute | solution.py:15
  90.3 5.7 %collective-permute-start.6 = (bf16[128,128]{1,0:T(8,128)(2,1)S(1)}, bf16[128,128]{1,0:T(8,128)(2,1)S(1)}, u32[]{:S(2)}, u32[]{:S(2)}) collective-permute-start(bf16[128,128]{1,0:T(8,128)(2,1)S(1)} %copy.97), channel_id=1, source_target_pairs={{0,4},{4,8},{8,12},{12,0},{1,5},{5,9},{9,13},{13,1},{2,6},{6,10},{... | collective-permute-start | bytes 98312 | tf_op jit(solution)/shard_map/while/body/eval_jaxpr/ppermute | solution.py:15
  91.4 5.7 %collective-permute-start.7 = (bf16[128,128]{1,0:T(8,128)(2,1)S(1)}, bf16[128,128]{1,0:T(8,128)(2,1)S(1)}, u32[]{:S(2)}, u32[]{:S(2)}) collective-permute-start(bf16[128,128]{1,0:T(8,128)(2,1)S(1)} %copy.98), channel_id=1, source_target_pairs={{0,4},{4,8},{8,12},{12,0},{1,5},{5,9},{9,13},{13,1},{2,6},{6,10},{... | collective-permute-start | bytes 98312 | tf_op jit(solution)/shard_map/while/body/eval_jaxpr/ppermute | solution.py:15
  98.4 6.1 %collective-permute-start.11 = (bf16[256,1,128]{2,0,1:T(8,128)(2,1)S(1)}, bf16[256,1,128]{2,0,1:T(8,128)(2,1)S(1)}, u32[]{:S(2)}, u32[]{:S(2)}) collective-permute-start(bf16[256,1,128]{2,0,1:T(8,128)(2,1)S(1)} %convert_element_type.122), channel_id=1, source_target_pairs={{0,4},{4,8},{8,12},{12,0},{1,5},{5,9},{9,13},{13,1},{2,6},{6,10},{... | collective-permute-start | bytes 196616 | tf_op jit(solution)/shard_map/ppermute | solution.py:15
  98.4 0.8 copy-start.12
  98.5 6.7 %collective-permute-start.10 = (bf16[256,1,128]{2,0,1:T(8,128)(2,1)S(1)}, bf16[256,1,128]{2,0,1:T(8,128)(2,1)S(1)}, u32[]{:S(2)}, u32[]{:S(2)}) collective-permute-start(bf16[256,1,128]{2,0,1:T(8,128)(2,1)S(1)} %convert_element_type.119), channel_id=1, source_target_pairs={{0,4},{4,8},{8,12},{12,0},{1,5},{5,9},{9,13},{13,1},{2,6},{6,10},{... | collective-permute-start | bytes 196616 | tf_op jit(solution)/shard_map/ppermute | solution.py:15
  104.5 0.7 copy-start.6
  105.2 0.6 copy-start.7
  105.8 76.9 %all-reduce.4.cloned.1.call-start = ((), (), s32[]{:S(2)}) async-start(), calls=%async_computation | async-start | bytes 131072 | tf_op jit(solution)/shard_map/psum | solution.py:208
  136.9 0.9 copy-start.13
  137.8 10.9 %copy-start.1 = (bf16[256,128]{1,0:T(8,128)(2,1)}, bf16[256,128]{1,0:T(8,128)(2,1)S(1)}, u32[]{:S(2)}) copy-start(bf16[256,128]{1,0:T(8,128)(2,1)S(1)} %fusion.71) | copy-start | bytes 196612
  148.7 34.0 %copy-start.5 = (bf16[256,128]{1,0:T(8,128)(2,1)S(1)}, bf16[256,128]{1,0:T(8,128)(2,1)}, u32[]{:S(2)}) copy-start(bf16[256,128]{1,0:T(8,128)(2,1)} %get-tuple-element.1577) | copy-start | bytes 196612
  182.7 0.9 copy-start.8
Sparse Core Ops, SparseCore 0:
  106.0 30.9 all-reduce.5
  148.8 33.8 all-reduce.3
where the time goes:
time: 190 us; the launch traced here: 191 us
  waiting for transfers between devices  54.1 us (28%)
  blocking collectives  46.2 us (24%)
  starting transfers between devices  32.9 us (17%)
  between operations  17.8 us (9%)
  loops' own time  12.8 us (7%)
  local copies, waits for them, and re-layouts  11.2 us (6%)
  matrix products  8.7 us (5%)
  other arithmetic  7.44 us (4%)
    ppermute x32, starting transfers between devices, passed_along(): return lax.ppermute(value, axis, pairs)  32.8 us
    ppermute x32, waiting for transfers between devices, passed_along(): return lax.ppermute(value, axis, pairs)  26.4 us
    psum x1, blocking collectives, on_device(): low_rank = lax.psum(low_partial, ('head', 'inner')).astype(jnp.bfloat16)  23.6 us
    psum x1, waiting for transfers between devices, on_device(): grad_a, grad_b = lax.psum((grad_a_part, grad_b_part), 'outer')  21.1 us
    psum x1, blocking collectives, on_device(): grad_a, grad_b = lax.psum((grad_a_part, grad_b_part), 'outer')  12.7 us
    psum x1, blocking collectives, on_device(): back_rank = lax.psum(back_partial, 'head').astype(jnp.bfloat16)  9.87 us
    psum x1, waiting for transfers between devices, on_device(): lax.psum(key_acc.astype(jnp.bfloat16), 'inner').astype(jnp.float32)  6.59 us
    another operation x1, loops' own time, on_device(): lax.fori_loop(0, cycle_size - 1, backward_turn, (local_keys, (empty_query...  6.28 us
  transfers between devices with their start and end apart: 34, of which 23 were waited for; matrix products, arithmetic and copies ran while one was open for 4% of the time, Pallas kernels for 0%

commit v1 on v0

v1 whole, which is shorter than its diff:
```python
import functools

import jax
import jax.numpy as jnp
from jax import lax
from jax.experimental import pallas as pl
from jax.experimental.pallas import tpu as pltpu
from jax.sharding import PartitionSpec as P

HEAD_DIM = 128
NEGATIVE = -1e30
MESH = pl.DeviceIdType.MESH
NT = (((1,), (1,)), ((), ()))
NN = (((1,), (0,)), ((), ()))
TN = (((0,), (0,)), ((), ()))


def mm(a, b, dims):
    return lax.dot_general(a, b, dims, preferred_element_type=jnp.float32)


def kernel(
    sizes,
    order_ref, docs_ref, q_hbm, k_hbm, v_hbm, g_hbm, hid_hbm, at_ref, b_ref,
    dq_ref, dk_ref, dv_ref, ga_ref, gb_ref,
    q_ref, g_ref, hid_ref, kv, st, dpt, dq_acc,
    low_out, low_in, rs1_out, rs1_in, rs2_out, rs2_in, fin, gbq, back_in, part_a, part_b,
    load_sem, kv_send, kv_recv, fw_send, low_send, low_recv,
    rs1_send, rs1_recv, rs2_send, rs2_recv, fin_send, fin_recv,
    gbq_send, gbq_recv, back_send, back_recv,
    pa_send, pa_recv, pb_send, pb_recv,
):
    nh, no, ni, heads = sizes
    h, o, i = lax.axis_index("head"), lax.axis_index("outer"), lax.axis_index("inner")
    rows = q_ref.shape[0]
    half = rows // 2
    part = rows // ni
    plane = nh * ni
    me = h * ni + i
    scaling = HEAD_DIM ** -0.5

    def at_outer(t):
        return lax.rem(o + t, no)

    def at_inner(t):
        return lax.rem(i + t, ni)

    def at_plane(t):
        return lax.rem(me + t, plane)

    def remote(src, dst, send, recv, dev):
        return pltpu.make_async_remote_copy(
            src_ref=src, dst_ref=dst, send_sem=send, recv_sem=recv, device_id=dev,
            device_id_type=MESH,
        )

    def plane_dev(p):
        return (p // ni, o, lax.rem(p, ni))

    kv_loads = []
    for j in range(ni):
        for which, src in enumerate((k_hbm, v_hbm)):
            kv_loads.append(
                pltpu.make_async_copy(
                    src.at[pl.ds(j * part, part)], kv.at[o, j, which],
                    load_sem.at[3 + 2 * j + which],
                )
            )
    q_load = pltpu.make_async_copy(q_hbm, q_ref, load_sem.at[0])
    g_load = pltpu.make_async_copy(g_hbm, g_ref, load_sem.at[1])
    hid_load = pltpu.make_async_copy(hid_hbm, hid_ref, load_sem.at[2])
    for copy in kv_loads + [hid_load, q_load, g_load]:
        copy.start()

    barrier = pltpu.get_barrier_semaphore()
    for t in range(1, no):
        pl.semaphore_signal(barrier, inc=1, device_id=(h, at_outer(t), i), device_id_type=MESH)
    for t in range(1, plane):
        pl.semaphore_signal(barrier, inc=1, device_id=plane_dev(at_plane(t)), device_id_type=MESH)
    pl.semaphore_wait(barrier, no - 1 + plane - 1)

    for copy in kv_loads:
        copy.wait()

    def kv_copy(t):
        return remote(kv.at[o, i], kv.at[o, i], kv_send.at[t], kv_recv.at[o, i],
                      (h, at_outer(t), i))

    def slot_wait(src, j):
        remote(kv.at[src, j], kv.at[src, j], kv_send.at[0], kv_recv.at[src, j],
               (h, at_outer(1), i)).wait_recv()

    def fw_copy(src, t, k):
        return remote(kv.at[src, i], kv.at[src, i], fw_send.at[t, k], kv_recv.at[src, i],
                      (h, o, at_inner(k)))

    for t in range(1, no):
        kv_copy(t).start()

    hid_load.wait()
    for j in range(ni):
        low_out[j] = mm(at_ref[...], hid_ref[j * part:(j + 1) * part, :], NT)
    low_in[me] = low_out[i]

    def low_copy(t):
        p = at_plane(t)
        return remote(low_out.at[lax.rem(p, ni)], low_in.at[me], low_send.at[t],
                      low_recv.at[me], plane_dev(p))

    for t in range(1, plane):
        low_copy(t).start()

    q_load.wait()
    g_load.wait()

    def row_meta(block):
        idx = order_ref[block]
        doc = docs_ref[pl.ds(idx, 1), :].astype(jnp.float32)
        return doc, idx * half

    lanes = lax.broadcasted_iota(jnp.int32, (1, half), 1)
    sublanes = lax.broadcasted_iota(jnp.int32, (half, rows), 0)
    qm = [row_meta(2 * o + b) for b in range(2)]
    q_doc = jnp.concatenate([m[0] for m in qm], 1)
    q_pos = jnp.concatenate([m[1] + lanes for m in qm], 1)

    def head_cols(x):
        return slice(x * HEAD_DIM, (x + 1) * HEAD_DIM)

    def block_scores(src, t, peaks):
        key_rows = kv[src, :, 0].reshape(rows, HEAD_DIM)
        val_rows = kv[src, :, 1].reshape(rows, HEAD_DIM)
        docs, poss = [], []
        for b in range(2):
            doc, first = row_meta(2 * src + b)
            wide = jnp.transpose(jnp.broadcast_to(doc, (half, half)))
            docs.append(jnp.concatenate([wide] * (rows // half), 1))
            poss.append(first + sublanes)
        seen = (jnp.concatenate(docs, 0) == q_doc) & (jnp.concatenate(poss, 0) <= q_pos)
        out = []
        for x in range(heads):
            s = mm(key_rows, q_ref[:, head_cols(x)], NT) * scaling
            s = jnp.where(seen, s, NEGATIVE)
            st[t, x] = s
            out.append(jnp.maximum(peaks[x], jnp.max(s, axis=0, keepdims=True)))
            dpt[t, x] = mm(val_rows, g_ref[:, head_cols(x)], NT)
        return tuple(out)

    peaks = tuple(jnp.full((1, rows), NEGATIVE, jnp.float32) for _ in range(heads))
    peaks = block_scores(o, 0, peaks)

    def forward(t):
        src = lax.rem(o - t + no, no)
        slot_wait(src, i)
        for k in range(1, ni):
            fw_copy(src, t, k).start()

    forward(1)

    def gather_step(t, peaks):
        @pl.when(t < no - 1)
        def _():
            forward(t + 1)

        src = lax.rem(o - t + no, no)
        for k in range(1, ni):
            slot_wait(src, at_inner(k))
        return block_scores(src, t, peaks)

    peaks = lax.fori_loop(1, no, gather_step, peaks)

    zero = jnp.zeros((1, rows), jnp.float32)

    def weigh_step(t, carried):
        out = []
        for x in range(heads):
            total, dot = carried[x]
            w = jnp.exp(st[t, x] - peaks[x])
            st[t, x] = w
            out.append((total + jnp.sum(w, axis=0, keepdims=True),
                        dot + jnp.sum(w * dpt[t, x], axis=0, keepdims=True)))
        return tuple(out)

    sums = lax.fori_loop(0, no, weigh_step, tuple((zero, zero) for _ in range(heads)))
    inv = [1.0 / total for total, _ in sums]
    delta = [dot * r for (_, dot), r in zip(sums, inv)]

    dq_acc[...] = jnp.zeros_like(dq_acc)

    def rs1_copy(src, k):
        return remote(rs1_out.at[src, at_inner(k)], rs1_in.at[src, i], rs1_send.at[src, k],
                      rs1_recv.at[src, i], (h, o, at_inner(k)))

    def grad_step(n, _):
        t = lax.rem(n + 1, no)
        src = lax.rem(o - t + no, no)
        key_rows = kv[src, :, 0].reshape(rows, HEAD_DIM)
        dk = jnp.zeros((rows, HEAD_DIM), jnp.float32)
        dv = jnp.zeros((rows, HEAD_DIM), jnp.float32)
        for x in range(heads):
            p = st[t, x] * inv[x]
            ds = (p * (dpt[t, x] - delta[x])).astype(jnp.bfloat16)
            dv += mm(p.astype(jnp.bfloat16), g_ref[:, head_cols(x)], NN)
            dk += mm(ds, q_ref[:, head_cols(x)], NN)
            dq_acc[:, head_cols(x)] += mm(ds, key_rows, TN)
        rs1_out[src, :, 0] = dk.astype(jnp.bfloat16).reshape(ni, part, HEAD_DIM)
        rs1_out[src, :, 1] = dv.astype(jnp.bfloat16).reshape(ni, part, HEAD_DIM)
        for k in range(1, ni):
            rs1_copy(src, k).start()
        return 0

    lax.fori_loop(0, no, grad_step, 0)
    dq_ref[...] = (dq_acc[...] * scaling).astype(jnp.bfloat16)

    def inner_sum(src):
        acc = rs1_out[src, i].astype(jnp.float32)
        for k in range(1, ni):
            j = at_inner(k)
            remote(rs1_in.at[src, j], rs1_in.at[src, j], rs1_send.at[src, k],
                   rs1_recv.at[src, j], (h, o, j)).wait_recv()
            acc = acc + rs1_in[src, j].astype(jnp.float32)
        return acc

    def rs2_copy(t):
        dst = lax.rem(o - t + no, no)
        return remote(rs2_out.at[t], rs2_in.at[o], rs2_send.at[t], rs2_recv.at[o], (h, dst, i))

    def home_step(t, _):
        rs2_out[t] = inner_sum(lax.rem(o - t + no, no)).astype(jnp.bfloat16)
        rs2_copy(t).start()
        return 0

    lax.fori_loop(1, no, home_step, 0)
    acc = inner_sum(o)
    for t in range(1, no):
        src = at_outer(t)
        remote(rs2_out.at[t], rs2_in.at[src], rs2_send.at[t], rs2_recv.at[src],
               (h, src, i)).wait_recv()
        acc = acc + rs2_in[src].astype(jnp.float32)
    dk_part = (acc[0] * scaling).astype(jnp.bfloat16)
    dv_part = acc[1].astype(jnp.bfloat16)
    back_in[me] = mm(b_ref[...], dk_part, NT)

    def back_copy(t):
        return remote(back_in.at[me], back_in.at[me], back_send.at[t], back_recv.at[me],
                      plane_dev(at_plane(t)))

    for t in range(1, plane):
        back_copy(t).start()
    fin[i, 0] = dk_part
    fin[i, 1] = dv_part

    low = low_in[me]
    for t in range(1, plane):
        p = at_plane(t)
        remote(low_out.at[0], low_in.at[p], low_send.at[t], low_recv.at[p],
               plane_dev(p)).wait_recv()
        low = low + low_in[p]
    gbq[i] = mm(low.astype(jnp.bfloat16), dk_part, NN)

    def fin_copy(k):
        return remote(fin.at[i], fin.at[i], fin_send.at[k], fin_recv.at[i], (h, o, at_inner(k)))

    def gbq_copy(k):
        return remote(gbq.at[i], gbq.at[i], gbq_send.at[k], gbq_recv.at[i], (h, o, at_inner(k)))

    for k in range(1, ni):
        gbq_copy(k).start()
        fin_copy(k).start()

    for t in range(1, plane):
        p = at_plane(t)
        remote(back_in.at[p], back_in.at[p], back_send.at[t], back_recv.at[p],
               plane_dev(p)).wait_recv()
    acc_a = jnp.zeros(ga_ref.shape, jnp.float32)
    for j in range(ni):
        back = back_in[j]
        for y in range(1, nh):
            back = back + back_in[y * ni + j]
        acc_a += mm(back.astype(jnp.bfloat16), hid_ref[j * part:(j + 1) * part, :], NN)
    part_a[o] = acc_a.astype(jnp.bfloat16)

    def pa_copy(t):
        return remote(part_a.at[o], part_a.at[o], pa_send.at[t], pa_recv.at[o],
                      (h, at_outer(t), i))

    def pb_copy(t):
        return remote(part_b.at[o], part_b.at[o], pb_send.at[t], pb_recv.at[o],
                      (h, at_outer(t), i))

    for t in range(1, no):
        pa_copy(t).start()

    for k in range(1, ni):
        j = at_inner(k)
        remote(gbq.at[j], gbq.at[j], gbq_send.at[k], gbq_recv.at[j], (h, o, j)).wait_recv()
    acc_b = gbq[0]
    for j in range(1, ni):
        acc_b = acc_b + gbq[j]
    part_b[o] = acc_b.astype(jnp.bfloat16)
    for t in range(1, no):
        pb_copy(t).start()

    for k in range(1, ni):
        j = at_inner(k)
        remote(fin.at[j], fin.at[j], fin_send.at[k], fin_recv.at[j], (h, o, j)).wait_recv()
    dk_ref[...] = fin[:, 0].reshape(rows, HEAD_DIM)
    dv_ref[...] = fin[:, 1].reshape(rows, HEAD_DIM)

    for t in range(1, no):
        kv_copy(t).wait_send()
        rs2_copy(t).wait_send()
        for k in range(1, ni):
            fw_copy(lax.rem(o - t + no, no), t, k).wait_send()
    for t in range(1, plane):
        low_copy(t).wait_send()
        back_copy(t).wait_send()
    for src in range(no):
        for k in range(1, ni):
            rs1_copy(src, k).wait_send()
    for k in range(1, ni):
        fin_copy(k).wait_send()
        gbq_copy(k).wait_send()

    for t in range(1, no):
        src = at_outer(t)
        remote(part_a.at[src], part_a.at[src], pa_send.at[t], pa_recv.at[src],
               (h, src, i)).wait_recv()
        remote(part_b.at[src], part_b.at[src], pb_send.at[t], pb_recv.at[src],
               (h, src, i)).wait_recv()
    total_a = part_a[0].astype(jnp.float32)
    total_b = part_b[0].astype(jnp.float32)
    for src in range(1, no):
        total_a += part_a[src].astype(jnp.float32)
        total_b += part_b[src].astype(jnp.float32)
    ga_ref[...] = total_a
    gb_ref[...] = total_b
    for t in range(1, no):
        pa_copy(t).wait_send()
        pb_copy(t).wait_send()


def on_device(
    sizes, queries, keys, values, grad_out, hidden_in, adapter_a, adapter_b, block_order, doc_ids
):
    nh, no, ni = sizes
    rows = queries.shape[0]
    half = rows // 2
    part = rows // ni
    width = hidden_in.shape[1]
    rank = adapter_a.shape[1]
    heads = queries.shape[1] // HEAD_DIM
    plane = nh * ni
    docs = doc_ids.reshape(-1, half)
    bf, f32 = jnp.bfloat16, jnp.float32
    dma = pltpu.SemaphoreType.DMA
    vmem = pl.BlockSpec(memory_space=pltpu.VMEM)
    hbm = pl.BlockSpec(memory_space=pl.ANY)
    share = (2, part, HEAD_DIM)
    grad_query, grad_key, grad_value, grad_a, grad_b = pl.pallas_call(
        functools.partial(kernel, (nh, no, ni, heads)),
        out_shape=(
            jax.ShapeDtypeStruct(queries.shape, bf),
            jax.ShapeDtypeStruct(keys.shape, bf),
            jax.ShapeDtypeStruct(values.shape, bf),
            jax.ShapeDtypeStruct((rank, width), f32),
            jax.ShapeDtypeStruct((rank, HEAD_DIM), f32),
        ),
        in_specs=[
            pl.BlockSpec(memory_space=pltpu.SMEM), vmem, hbm, hbm, hbm, hbm, hbm, vmem, vmem,
        ],
        out_specs=(vmem,) * 5,
        scratch_shapes=[
            pltpu.VMEM(queries.shape, bf),
            pltpu.VMEM(queries.shape, bf),
            pltpu.VMEM((rows, width), bf),
            pltpu.VMEM((no, ni) + share, bf),
            pltpu.VMEM((no, heads, rows, rows), f32),
            pltpu.VMEM((no, heads, rows, rows), f32),
            pltpu.VMEM(queries.shape, f32),
            pltpu.VMEM((ni, rank, part), f32),
            pltpu.VMEM((plane, rank, part), f32),
            pltpu.VMEM((no, ni) + share, bf),
            pltpu.VMEM((no, ni) + share, bf),
            pltpu.VMEM((no,) + share, bf),
            pltpu.VMEM((no,) + share, bf),
            pltpu.VMEM((ni,) + share, bf),
            pltpu.VMEM((ni, rank, HEAD_DIM), f32),
            pltpu.VMEM((plane, rank, part), f32),
            pltpu.VMEM((no, rank, width), bf),
            pltpu.VMEM((no, rank, HEAD_DIM), bf),
            dma((3 + 2 * ni,)),
            dma((no,)), dma((no, ni)), dma((no, ni)),
            dma((plane,)), dma((plane,)),
            dma((no, ni)), dma((no, ni)),
            dma((no,)), dma((no,)),
            dma((ni,)), dma((ni,)),
            dma((ni,)), dma((ni,)),
            dma((plane,)), dma((plane,)),
            dma((no,)), dma((no,)),
            dma((no,)), dma((no,)),
        ],
        compiler_params=pltpu.CompilerParams(
            collective_id=0, has_side_effects=True, vmem_limit_bytes=60 * 1024 * 1024
        ),
    )(block_order, docs, queries, keys, values, grad_out, hidden_in, adapter_a.T, adapter_b)
    return grad_query, grad_key, grad_value, grad_a.T, grad_b


def solution(mesh):
    sizes = tuple(mesh.shape[name] for name in ("head", "outer", "inner"))
    in_specs = (
        P("outer", ("head", "inner")),
        P("outer", "head"),
        P("outer", "head"),
        P("outer", ("head", "inner")),
        P("outer", ("head", "inner")),
        P(("head", "inner"), None),
        P(None, "head"),
        P(),
        P(),
    )
    out_specs = (
        P("outer", ("head", "inner")),
        P("outer", "head"),
        P("outer", "head"),
        P(("head", "inner"), None),
        P(None, "head"),
    )
    return jax.shard_map(
        functools.partial(on_device, sizes),
        mesh=mesh, in_specs=in_specs, out_specs=out_specs, check_vma=False,
    )
```

time: 190 us -> 43.6 us (0.23)
  waiting for transfers between devices: 54.1 us -> 0 us
  blocking collectives: 46.2 us -> 0 us
  Pallas kernels: 0 us -> 38 us
  starting transfers between devices: 32.9 us -> 0 us
  between operations: 17.8 us -> 0.66 us
  loops' own time: 12.8 us -> 0 us
  matrix products: 8.7 us -> 0 us
  other arithmetic: 7.44 us -> 0 us
  local copies, waits for them, and re-layouts: 11.2 us -> 4.62 us
    psum x3 -> x0, blocking collectives: 46.2 us -> none  [the longest x1 23.6 us: on_device(): low_rank = lax.psum(low_partial, ('head', 'inner')).astype(jnp.bfloat16)]
    pallas_call x0 -> x1, Pallas kernels: none -> 38 us  [on_device(): pl.pallas_call(functools.partial(kernel, (nh, no, ni, heads)), out_shape=...]
    ppermute x32 -> x0, starting transfers between devices: 32.8 us -> none  [passed_along(): return lax.ppermute(value, axis, pairs)]
    psum x2 -> x0, waiting for transfers between devices: 27.7 us -> none  [the longest x1 21.1 us: on_device(): grad_a, grad_b = lax.psum((grad_a_part, grad_b_part), 'outer')]
    ppermute x32 -> x0, waiting for transfers between devices: 26.4 us -> none  [passed_along(): return lax.ppermute(value, axis, pairs)]
    another operation x10 -> x0, loops' own time: 12.8 us -> none  [the longest x1 6.28 us: on_device(): lax.fori_loop(0, cycle_size - 1, backward_turn, (local_keys, (empty_query...]
    dot_general x32 -> x0, matrix products: 8.7 us -> none  [the longest x8 2 us: tile_scores(): jnp.einsum('tkgd,skd->kgts', query_tile, key_rows, preferred_element_type...]
    reduce_or x7 -> x0, other arithmetic: 5.41 us -> none  [sweep(): return lax.cond(jnp.any(masked), active, resting, carried)]
  transfers between devices with their start and end apart: 34 -> 0, of which waited for: 23 -> 0; matrix products, arithmetic and copies ran while one was open for 4% -> 0% of each run, Pallas kernels for 0% -> 0%
where the time goes in v1:
time: 43.6 us; the launch traced here: 43.3 us
  Pallas kernels  38 us (87%)
  local copies, waits for them, and re-layouts  4.62 us (11%)
  between operations  0.66 us (2%)
    pallas_call x1, Pallas kernels, on_device(): pl.pallas_call(functools.partial(kernel, (nh, no, ni, heads)), out_shape=...  38 us
    unnamed x13, local copies, waits for them, and re-layouts  4.62 us

profile of v1, /device:TPU:0, one launch (start us, length us, event | category | flops | bytes accessed | tf_op | source)
XLA Modules:
  0.0 43.3 jit_solution(3647032470119056675)
XLA Ops:
  0.6 38.0 %shard_map.128 = (bf16[256,256]{1,0:T(8,128)(2,1)}, bf16[256,128]{1,0:T(8,128)(2,1)}, bf16[256,128]{1,0:T(8,128)(2,1)}, f32[16,1024]{1,0:T(8,128)}, f32[16,128]{1,0:T(8,128)}) custom-call(s32[8]{0:T(128)} %order_ref.1, s32[8,128]{1,0:T(8,128)} %bitcast.5, bf16[256,256]{1,0:T(8,128)(2,1)} %q_hbm.1, bf16[256,128]{1,0:T(8,128)(2,1)} %k_hbm.1, ...), custom_call_target="tpu_custom_call" | custom-call | tf_op jit(solution)/shard_map/pallas_call | solution.py:360
  38.7 0.0 copy-start.2
  38.7 1.6 %copy.19 = bf16[256,256]{1,0:T(8,128)(2,1)} copy(bf16[256,256]{1,0:T(8,128)(2,1)} %get-tuple-element.20) | data formatting | bytes 262144
  40.3 0.0 copy-done.2
  40.3 0.0 copy-start.1
  40.3 0.6 %copy.20 = bf16[256,128]{1,0:T(8,128)(2,1)} copy(bf16[256,128]{1,0:T(8,128)(2,1)S(1)} %copy-done.2) | data formatting | bytes 131072
  40.9 0.2 copy-done.1
  41.1 0.0 copy-start
  41.1 0.6 %copy.21 = bf16[256,128]{1,0:T(8,128)(2,1)} copy(bf16[256,128]{1,0:T(8,128)(2,1)S(1)} %copy-done.1) | data formatting | bytes 131072
  41.8 0.2 copy-done
  42.0 0.0 copy-start.3
  42.0 0.6 %copy.22 = f32[1024,16]{0,1:T(8,128)} copy(f32[1024,16]{0,1:T(8,128)S(1)} %bitcast.3) | data formatting | bytes 131072
  42.6 0.1 copy-done.3
  42.7 0.6 %copy.23 = f32[16,128]{1,0:T(8,128)} copy(f32[16,128]{1,0:T(8,128)S(1)} %copy-done.3) | data formatting | bytes 16384
Async XLA Ops:
  38.7 1.6 %copy-start.2 = (bf16[256,128]{1,0:T(8,128)(2,1)S(1)}, bf16[256,128]{1,0:T(8,128)(2,1)}, u32[]{:S(2)}) copy-start(bf16[256,128]{1,0:T(8,128)(2,1)} %get-tuple-element.21) | copy-start | bytes 196612
  40.3 0.9 %copy-start.1 = (bf16[256,128]{1,0:T(8,128)(2,1)S(1)}, bf16[256,128]{1,0:T(8,128)(2,1)}, u32[]{:S(2)}) copy-start(bf16[256,128]{1,0:T(8,128)(2,1)} %get-tuple-element.22) | copy-start | bytes 196612
  41.1 0.9 %copy-start = (f32[16,1024]{1,0:T(8,128)S(1)}, f32[16,1024]{1,0:T(8,128)}, u32[]{:S(2)}) copy-start(f32[16,1024]{1,0:T(8,128)} %get-tuple-element.13) | copy-start | bytes 196612
  42.0 0.7 %copy-start.3 = (f32[16,128]{1,0:T(8,128)S(1)}, f32[16,128]{1,0:T(8,128)}, u32[]{:S(2)}) copy-start(f32[16,128]{1,0:T(8,128)} %get-tuple-element.24) | copy-start | bytes 24580

commit v2 on v1

--- a/solution.py
+++ b/solution.py
@@ -24,10 +24,11 @@
     order_ref, docs_ref, q_hbm, k_hbm, v_hbm, g_hbm, hid_hbm, at_ref, b_ref,
     dq_ref, dk_ref, dv_ref, ga_ref, gb_ref,
     q_ref, g_ref, hid_ref, kv, st, dpt, dq_acc,
-    low_out, low_in, rs1_out, rs1_in, rs2_out, rs2_in, fin, gbq, back_in, part_a, part_b,
-    load_sem, kv_send, kv_recv, fw_send, low_send, low_recv,
+    low_out, low_in, low_all, rs1_out, rs1_in, rs2_out, rs2_in, fin, gbq, zb_out, zb_in, back_in,
+    part_a, part_b,
+    load_sem, kv_send, kv_recv, fx_send, fs_send, low_send, low_recv, la_send, la_recv,
     rs1_send, rs1_recv, rs2_send, rs2_recv, fin_send, fin_recv,
-    gbq_send, gbq_recv, back_send, back_recv,
+    gbq_send, gbq_recv, zb_send, zb_recv, back_send, back_recv,
     pa_send, pa_recv, pb_send, pb_recv,
 ):
     nh, no, ni, heads = sizes
@@ -90,9 +91,19 @@
         remote(kv.at[src, j], kv.at[src, j], kv_send.at[0], kv_recv.at[src, j],
                (h, at_outer(1), i)).wait_recv()
 
-    def fw_copy(src, t, k):
-        return remote(kv.at[src, i], kv.at[src, i], fw_send.at[t, k], kv_recv.at[src, i],
-                      (h, o, at_inner(k)))
+    sibling = i + 1 - 2 * lax.rem(i, 2)
+
+    def cross(k):
+        return at_inner(2 * k)
+
+    def cross_copy(src, t, k):
+        return remote(kv.at[src, i], kv.at[src, i], fx_send.at[t, k], kv_recv.at[src, i],
+                      (h, o, cross(k)))
+
+    def sibling_copy(src, t, k):
+        j = cross(k)
+        return remote(kv.at[src, j], kv.at[src, j], fs_send.at[t, k], kv_recv.at[src, j],
+                      (h, o, sibling))
 
     for t in range(1, no):
         kv_copy(t).start()
@@ -152,8 +163,9 @@
     def forward(t):
         src = lax.rem(o - t + no, no)
         slot_wait(src, i)
-        for k in range(1, ni):
-            fw_copy(src, t, k).start()
+        for k in range(1, ni // 2):
+            cross_copy(src, t, k).start()
+        sibling_copy(src, t, 0).start()
 
     forward(1)
 
@@ -163,11 +175,29 @@
             forward(t + 1)
 
         src = lax.rem(o - t + no, no)
-        for k in range(1, ni):
-            slot_wait(src, at_inner(k))
+        for k in range(1, ni // 2):
+            slot_wait(src, cross(k))
+            sibling_copy(src, t, k).start()
+        for k in range(ni // 2):
+            slot_wait(src, lax.rem(sibling + 2 * k, ni))
         return block_scores(src, t, peaks)
 
     peaks = lax.fori_loop(1, no, gather_step, peaks)
+
+    low = low_in[me]
+    for t in range(1, plane):
+        p = at_plane(t)
+        remote(low_out.at[0], low_in.at[p], low_send.at[t], low_recv.at[p],
+               plane_dev(p)).wait_recv()
+        low = low + low_in[p]
+    low_all[o] = low.astype(jnp.bfloat16)
+
+    def la_copy(t):
+        return remote(low_all.at[o], low_all.at[o], la_send.at[t], la_recv.at[o],
+                      (h, at_outer(t), i))
+
+    for t in range(1, no):
+        la_copy(t).start()
 
     zero = jnp.zeros((1, rows), jnp.float32)
 
@@ -190,6 +220,10 @@
     def rs1_copy(src, k):
         return remote(rs1_out.at[src, at_inner(k)], rs1_in.at[src, i], rs1_send.at[src, k],
                       rs1_recv.at[src, i], (h, o, at_inner(k)))
+
+    def zb_copy(t):
+        dst = lax.rem(o - t + no, no)
+        return remote(zb_out.at[t], zb_in.at[o], zb_send.at[t], zb_recv.at[o], (h, dst, i))
 
     def grad_step(n, _):
         t = lax.rem(n + 1, no)
@@ -207,10 +241,37 @@
         rs1_out[src, :, 1] = dv.astype(jnp.bfloat16).reshape(ni, part, HEAD_DIM)
         for k in range(1, ni):
             rs1_copy(src, k).start()
+        back = mm(b_ref[...], dk.astype(jnp.bfloat16), NT) * scaling
+        zb_out[t] = back.astype(jnp.bfloat16)
+
+        @pl.when(t > 0)
+        def _():
+            zb_copy(t).start()
+
         return 0
 
     lax.fori_loop(0, no, grad_step, 0)
     dq_ref[...] = (dq_acc[...] * scaling).astype(jnp.bfloat16)
+
+    acc = zb_out[0].astype(jnp.float32)
+    for t in range(1, no):
+        src = at_outer(t)
+        remote(zb_out.at[t], zb_in.at[src], zb_send.at[t], zb_recv.at[src],
+               (h, src, i)).wait_recv()
+        acc = acc + zb_in[src].astype(jnp.float32)
+    back_in[me] = acc.astype(jnp.bfloat16)
+
+    def back_copy(t):
+        return remote(back_in.at[me], back_in.at[me], back_send.at[t], back_recv.at[me],
+                      plane_dev(at_plane(t)))
+
+    for t in range(1, plane):
+        back_copy(t).start()
+
+    for t in range(1, no):
+        src = at_outer(t)
+        remote(low_all.at[src], low_all.at[src], la_send.at[t], la_recv.at[src],
+               (h, src, i)).wait_recv()
 
     def inner_sum(src):
         acc = rs1_out[src, i].astype(jnp.float32)
@@ -225,38 +286,46 @@
         dst = lax.rem(o - t + no, no)
         return remote(rs2_out.at[t], rs2_in.at[o], rs2_send.at[t], rs2_recv.at[o], (h, dst, i))
 
-    def home_step(t, _):
-        rs2_out[t] = inner_sum(lax.rem(o - t + no, no)).astype(jnp.bfloat16)
+    def home_step(t, acc_b):
+        src = lax.rem(o - t + no, no)
+        rs2_out[t] = inner_sum(src).astype(jnp.bfloat16)
         rs2_copy(t).start()
-        return 0
-
-    lax.fori_loop(1, no, home_step, 0)
+        return acc_b + mm(low_all[src], rs2_out[t, 0], NN)
+
+    acc_b = lax.fori_loop(1, no, home_step, jnp.zeros(gb_ref.shape, jnp.float32))
     acc = inner_sum(o)
+    acc_b = acc_b + mm(low_all[o], acc[0].astype(jnp.bfloat16), NN)
+    part_b[o] = (acc_b * scaling).astype(jnp.bfloat16)
+
+    def pa_copy(t):
+        return remote(part_a.at[o], part_a.at[o], pa_send.at[t], pa_recv.at[o],
+                      (h, at_outer(t), i))
+
+    def pb_copy(t):
+        return remote(part_b.at[o], part_b.at[o], pb_send.at[t], pb_recv.at[o],
+                      (h, at_outer(t), i))
+
+    for t in range(1, no):
+        pb_copy(t).start()
+
+    back = jnp.zeros((ga_ref.shape[0], rows), jnp.float32)
+    for t in range(1, plane):
+        p = at_plane(t)
+        remote(back_in.at[p], back_in.at[p], back_send.at[t], back_recv.at[p],
+               plane_dev(p)).wait_recv()
+    for p in range(plane):
+        back = back + back_in[p].astype(jnp.float32)
+    part_a[o] = mm(back.astype(jnp.bfloat16), hid_ref[...], NN).astype(jnp.bfloat16)
+    for t in range(1, no):
+        pa_copy(t).start()
+
     for t in range(1, no):
         src = at_outer(t)
         remote(rs2_out.at[t], rs2_in.at[src], rs2_send.at[t], rs2_recv.at[src],
                (h, src, i)).wait_recv()
         acc = acc + rs2_in[src].astype(jnp.float32)
-    dk_part = (acc[0] * scaling).astype(jnp.bfloat16)
-    dv_part = acc[1].astype(jnp.bfloat16)
-    back_in[me] = mm(b_ref[...], dk_part, NT)
-
-    def back_copy(t):
-        return remote(back_in.at[me], back_in.at[me], back_send.at[t], back_recv.at[me],
-                      plane_dev(at_plane(t)))
-
-    for t in range(1, plane):
-        back_copy(t).start()
-    fin[i, 0] = dk_part
-    fin[i, 1] = dv_part
-
-    low = low_in[me]
-    for t in range(1, plane):
-        p = at_plane(t)
-        remote(low_out.at[0], low_in.at[p], low_send.at[t], low_recv.at[p],
-               plane_dev(p)).wait_recv()
-        low = low + low_in[p]
-    gbq[i] = mm(low.astype(jnp.bfloat16), dk_part, NN)
+    fin[i, 0] = (acc[0] * scaling).astype(jnp.bfloat16)
+    fin[i, 1] = acc[1].astype(jnp.bfloat16)
 
     def fin_copy(k):
         return remote(fin.at[i], fin.at[i], fin_send.at[k], fin_recv.at[i], (h, o, at_inner(k)))
@@ -265,53 +334,41 @@
         return remote(gbq.at[i], gbq.at[i], gbq_send.at[k], gbq_recv.at[i], (h, o, at_inner(k)))
 
     for k in range(1, ni):
+        fin_copy(k).start()
+
+    for t in range(1, no):
+        src = at_outer(t)
+        remote(part_b.at[src], part_b.at[src], pb_send.at[t], pb_recv.at[src],
+               (h, src, i)).wait_recv()
+    total_b = part_b[0].astype(jnp.float32)
+    for src in range(1, no):
+        total_b += part_b[src].astype(jnp.float32)
+    gbq[i] = total_b
+    for k in range(1, ni):
         gbq_copy(k).start()
-        fin_copy(k).start()
-
-    for t in range(1, plane):
-        p = at_plane(t)
-        remote(back_in.at[p], back_in.at[p], back_send.at[t], back_recv.at[p],
-               plane_dev(p)).wait_recv()
-    acc_a = jnp.zeros(ga_ref.shape, jnp.float32)
-    for j in range(ni):
-        back = back_in[j]
-        for y in range(1, nh):
-            back = back + back_in[y * ni + j]
-        acc_a += mm(back.astype(jnp.bfloat16), hid_ref[j * part:(j + 1) * part, :], NN)
-    part_a[o] = acc_a.astype(jnp.bfloat16)
-
-    def pa_copy(t):
-        return remote(part_a.at[o], part_a.at[o], pa_send.at[t], pa_recv.at[o],
-                      (h, at_outer(t), i))
-
-    def pb_copy(t):
-        return remote(part_b.at[o], part_b.at[o], pb_send.at[t], pb_recv.at[o],
-                      (h, at_outer(t), i))
-
-    for t in range(1, no):
-        pa_copy(t).start()
-
-    for k in range(1, ni):
-        j = at_inner(k)
-        remote(gbq.at[j], gbq.at[j], gbq_send.at[k], gbq_recv.at[j], (h, o, j)).wait_recv()
-    acc_b = gbq[0]
-    for j in range(1, ni):
-        acc_b = acc_b + gbq[j]
-    part_b[o] = acc_b.astype(jnp.bfloat16)
-    for t in range(1, no):
-        pb_copy(t).start()
 
     for k in range(1, ni):
         j = at_inner(k)
         remote(fin.at[j], fin.at[j], fin_send.at[k], fin_recv.at[j], (h, o, j)).wait_recv()
     dk_ref[...] = fin[:, 0].reshape(rows, HEAD_DIM)
     dv_ref[...] = fin[:, 1].reshape(rows, HEAD_DIM)
+    for k in range(1, ni):
+        j = at_inner(k)
+        remote(gbq.at[j], gbq.at[j], gbq_send.at[k], gbq_recv.at[j], (h, o, j)).wait_recv()
+    total_b = gbq[0]
+    for j in range(1, ni):
+        total_b = total_b + gbq[j]
+    gb_ref[...] = total_b
 
     for t in range(1, no):
         kv_copy(t).wait_send()
         rs2_copy(t).wait_send()
-        for k in range(1, ni):
-            fw_copy(lax.rem(o - t + no, no), t, k).wait_send()
+        zb_copy(t).wait_send()
+        la_copy(t).wait_send()
+        for k in range(ni // 2):
+            if k:
+                cross_copy(lax.rem(o - t + no, no), t, k).wait_send()
+            sibling_copy(lax.rem(o - t + no, no), t, k).wait_send()
     for t in range(1, plane):
         low_copy(t).wait_send()
         back_copy(t).wait_send()
@@ -326,18 +383,25 @@
         src = at_outer(t)
         remote(part_a.at[src], part_a.at[src], pa_send.at[t], pa_recv.at[src],
                (h, src, i)).wait_recv()
-        remote(part_b.at[src], part_b.at[src], pb_send.at[t], pb_recv.at[src],
-               (h, src, i)).wait_recv()
     total_a = part_a[0].astype(jnp.float32)
-    total_b = part_b[0].astype(jnp.float32)
     for src in range(1, no):
         total_a += part_a[src].astype(jnp.float32)
-        total_b += part_b[src].astype(jnp.float32)
     ga_ref[...] = total_a
-    gb_ref[...] = total_b
     for t in range(1, no):
         pa_copy(t).wait_send()
         pb_copy(t).wait_send()
+
+
+def put_out(*refs):
+    count = len(refs) // 2
+    sem = refs[-1]
+    copies = [
+        pltpu.make_async_copy(refs[n], refs[count + n], sem.at[n]) for n in range(count)
+    ]
+    for copy in copies:
+        copy.start()
+    for copy in copies:
+        copy.wait()
 
 
 def on_device(
@@ -357,15 +421,16 @@
     vmem = pl.BlockSpec(memory_space=pltpu.VMEM)
     hbm = pl.BlockSpec(memory_space=pl.ANY)
     share = (2, part, HEAD_DIM)
-    grad_query, grad_key, grad_value, grad_a, grad_b = pl.pallas_call(
+    results = (
+        (queries.shape, bf),
+        (keys.shape, bf),
+        (values.shape, bf),
+        ((rank, width), f32),
+        ((rank, HEAD_DIM), f32),
+    )
+    held = pl.pallas_call(
         functools.partial(kernel, (nh, no, ni, heads)),
-        out_shape=(
-            jax.ShapeDtypeStruct(queries.shape, bf),
-            jax.ShapeDtypeStruct(keys.shape, bf),
-            jax.ShapeDtypeStruct(values.shape, bf),
-            jax.ShapeDtypeStruct((rank, width), f32),
-            jax.ShapeDtypeStruct((rank, HEAD_DIM), f32),
-        ),
+        out_shape=tuple(pltpu.VMEM(*result) for result in results),
         in_specs=[
             pl.BlockSpec(memory_space=pltpu.SMEM), vmem, hbm, hbm, hbm, hbm, hbm, vmem, vmem,
         ],
@@ -380,22 +445,25 @@
             pltpu.VMEM(queries.shape, f32),
             pltpu.VMEM((ni, rank, part), f32),
             pltpu.VMEM((plane, rank, part), f32),
+            pltpu.VMEM((no, rank, part), bf),
             pltpu.VMEM((no, ni) + share, bf),
             pltpu.VMEM((no, ni) + share, bf),
             pltpu.VMEM((no,) + share, bf),
             pltpu.VMEM((no,) + share, bf),
             pltpu.VMEM((ni,) + share, bf),
             pltpu.VMEM((ni, rank, HEAD_DIM), f32),
-            pltpu.VMEM((plane, rank, part), f32),
+            pltpu.VMEM((no, rank, rows), bf),
+            pltpu.VMEM((no, rank, rows), bf),
+            pltpu.VMEM((plane, rank, rows), bf),
             pltpu.VMEM((no, rank, width), bf),
             pltpu.VMEM((no, rank, HEAD_DIM), bf),
             dma((3 + 2 * ni,)),
-            dma((no,)), dma((no, ni)), dma((no, ni)),
-            dma((plane,)), dma((plane,)),
+            dma((no,)), dma((no, ni)), dma((no, ni // 2)), dma((no, ni // 2)),
+            dma((plane,)), dma((plane,)), dma((no,)), dma((no,)),
             dma((no, ni)), dma((no, ni)),
             dma((no,)), dma((no,)),
             dma((ni,)), dma((ni,)),
-            dma((ni,)), dma((ni,)),
+            dma((ni,)), dma((ni,)), dma((no,)), dma((no,)),
             dma((plane,)), dma((plane,)),
             dma((no,)), dma((no,)),
             dma((no,)), dma((no,)),
@@ -404,6 +472,14 @@
             collective_id=0, has_side_effects=True, vmem_limit_bytes=60 * 1024 * 1024
         ),
     )(block_order, docs, queries, keys, values, grad_out, hidden_in, adapter_a.T, adapter_b)
+    grad_query, grad_key, grad_value, grad_a, grad_b = pl.pallas_call(
+        put_out,
+        out_shape=tuple(jax.ShapeDtypeStruct(*result) for result in results),
+        in_specs=[vmem] * len(results),
+        out_specs=(hbm,) * len(results),
+        scratch_shapes=[dma((len(results),))],
+        compiler_params=pltpu.CompilerParams(vmem_limit_bytes=8 * 1024 * 1024),
+    )(*held)
     return grad_query, grad_key, grad_value, grad_a.T, grad_b
 
 

time: 43.6 us -> 34.7 us (0.80)
  local copies, waits for them, and re-layouts: 4.62 us -> 0 us
  Pallas kernels: 38 us -> 33.8 us
    pallas_call x1, Pallas kernels: 38 us -> 33.1 us  [on_device(): pl.pallas_call(functools.partial(kernel, (nh, no, ni, heads)), out_shape=...]
    unnamed x13 -> x0, local copies, waits for them, and re-layouts: 4.62 us -> none
    pallas_call x0 -> x1, Pallas kernels: none -> 0.76 us  [on_device(): pl.pallas_call(put_out, out_shape=tuple((jax.ShapeDtypeStruct(*result) fo...]
where the time goes in v2:
time: 34.7 us; the launch traced here: 34.5 us
  Pallas kernels  33.8 us (97%)
  between operations  0.64 us (2%)
    pallas_call x1, Pallas kernels, on_device(): pl.pallas_call(functools.partial(kernel, (nh, no, ni, heads)), out_shape=...  33.1 us
    pallas_call x1, Pallas kernels, on_device(): pl.pallas_call(put_out, out_shape=tuple((jax.ShapeDtypeStruct(*result) fo...  0.76 us

profile of v2, /device:TPU:0, one launch (start us, length us, event | category | flops | bytes accessed | tf_op | source)
XLA Modules:
  0.0 34.5 jit_solution(13552587197797072729)
XLA Ops:
  0.6 33.1 %shard_map.128 = (bf16[256,256]{1,0:T(8,128)(2,1)S(1)}, bf16[256,128]{1,0:T(8,128)(2,1)S(1)}, bf16[256,128]{1,0:T(8,128)(2,1)S(1)}, f32[16,1024]{1,0:T(8,128)S(1)}, f32[16,128]{1,0:T(8,128)S(1)}) custom-call(s32[8]{0:T(128)} %order_ref.1, s32[8,128]{1,0:T(8,128)} %bitcast.4, bf16[256,256]{1,0:T(8,128)(2,1)} %q_hbm.1, bf16[256,128]{1,0:T(8,128)(2,1)} %k_hbm.1, ...), custom_call_target="tpu_custom_call" | custom-call | tf_op jit(solution)/shard_map/pallas_call | solution.py:431
  33.7 0.8 %shard_map.129 = (bf16[256,256]{1,0:T(8,128)(2,1)}, bf16[256,128]{1,0:T(8,128)(2,1)}, bf16[256,128]{1,0:T(8,128)(2,1)}, f32[16,1024]{1,0:T(8,128)}, f32[16,128]{1,0:T(8,128)}) custom-call(bf16[256,256]{1,0:T(8,128)(2,1)S(1)} %get-tuple-element.15.refs_0_, bf16[256,128]{1,0:T(8,128)(2,1)S(1)} %get-tuple-element.16.refs_1_, ...), custom_call_target="tpu_custom_call" | custom-call | tf_op jit(solution)/shard_map/pallas_call | solution.py:475

commit v3 on v2

--- a/solution.py
+++ b/solution.py
@@ -24,10 +24,10 @@
     order_ref, docs_ref, q_hbm, k_hbm, v_hbm, g_hbm, hid_hbm, at_ref, b_ref,
     dq_ref, dk_ref, dv_ref, ga_ref, gb_ref,
     q_ref, g_ref, hid_ref, kv, st, dpt, dq_acc,
-    low_out, low_in, low_all, rs1_out, rs1_in, rs2_out, rs2_in, fin, gbq, zb_out, zb_in, back_in,
+    low_out, low_in, low_all, rs1_out, rs1_in, rsx_out, rsx_in, rs2_out, rs2_in, fin, gbq, zb_out, zb_in, back_in,
     part_a, part_b,
     load_sem, kv_send, kv_recv, fx_send, fs_send, low_send, low_recv, la_send, la_recv,
-    rs1_send, rs1_recv, rs2_send, rs2_recv, fin_send, fin_recv,
+    rs1_send, rs1_recv, rsx_send, rsx_recv, rs2_send, rs2_recv, fin_send, fin_recv,
     gbq_send, gbq_recv, zb_send, zb_recv, back_send, back_recv,
     pa_send, pa_recv, pb_send, pb_recv,
 ):
@@ -218,8 +218,23 @@
     dq_acc[...] = jnp.zeros_like(dq_acc)
 
     def rs1_copy(src, k):
-        return remote(rs1_out.at[src, at_inner(k)], rs1_in.at[src, i], rs1_send.at[src, k],
-                      rs1_recv.at[src, i], (h, o, at_inner(k)))
+        j = lax.rem(sibling + 2 * k, ni)
+        return remote(rs1_out.at[src, j], rs1_in.at[src, j], rs1_send.at[src, k],
+                      rs1_recv.at[src, j], (h, o, sibling))
+
+    def rsx_copy(src, k):
+        return remote(rsx_out.at[src, k], rsx_in.at[src, i], rsx_send.at[src, k],
+                      rsx_recv.at[src, i], (h, o, cross(k)))
+
+    def pair_step(src):
+        for k in reversed(range(ni // 2)):
+            j = cross(k)
+            remote(rs1_out.at[src, j], rs1_in.at[src, j], rs1_send.at[src, k],
+                   rs1_recv.at[src, j], (h, o, sibling)).wait_recv()
+            if k:
+                pair = rs1_out[src, j].astype(jnp.float32) + rs1_in[src, j].astype(jnp.float32)
+                rsx_out[src, k] = pair.astype(jnp.bfloat16)
+                rsx_copy(src, k).start()
 
     def zb_copy(t):
         dst = lax.rem(o - t + no, no)
@@ -239,7 +254,7 @@
             dq_acc[:, head_cols(x)] += mm(ds, key_rows, TN)
         rs1_out[src, :, 0] = dk.astype(jnp.bfloat16).reshape(ni, part, HEAD_DIM)
         rs1_out[src, :, 1] = dv.astype(jnp.bfloat16).reshape(ni, part, HEAD_DIM)
-        for k in range(1, ni):
+        for k in reversed(range(ni // 2)):
             rs1_copy(src, k).start()
         back = mm(b_ref[...], dk.astype(jnp.bfloat16), NT) * scaling
         zb_out[t] = back.astype(jnp.bfloat16)
@@ -248,9 +263,14 @@
         def _():
             zb_copy(t).start()
 
+        @pl.when(n > 0)
+        def _():
+            pair_step(lax.rem(o - n + no, no))
+
         return 0
 
     lax.fori_loop(0, no, grad_step, 0)
+    pair_step(o)
     dq_ref[...] = (dq_acc[...] * scaling).astype(jnp.bfloat16)
 
     acc = zb_out[0].astype(jnp.float32)
@@ -274,12 +294,12 @@
                (h, src, i)).wait_recv()
 
     def inner_sum(src):
-        acc = rs1_out[src, i].astype(jnp.float32)
-        for k in range(1, ni):
-            j = at_inner(k)
-            remote(rs1_in.at[src, j], rs1_in.at[src, j], rs1_send.at[src, k],
-                   rs1_recv.at[src, j], (h, o, j)).wait_recv()
-            acc = acc + rs1_in[src, j].astype(jnp.float32)
+        acc = rs1_out[src, i].astype(jnp.float32) + rs1_in[src, i].astype(jnp.float32)
+        for k in range(1, ni // 2):
+            j = cross(k)
+            remote(rsx_out.at[src, k], rsx_in.at[src, j], rsx_send.at[src, k],
+                   rsx_recv.at[src, j], (h, o, j)).wait_recv()
+            acc = acc + rsx_in[src, j].astype(jnp.float32)
         return acc
 
     def rs2_copy(t):
@@ -373,8 +393,10 @@
         low_copy(t).wait_send()
         back_copy(t).wait_send()
     for src in range(no):
-        for k in range(1, ni):
+        for k in range(ni // 2):
             rs1_copy(src, k).wait_send()
+            if k:
+                rsx_copy(src, k).wait_send()
     for k in range(1, ni):
         fin_copy(k).wait_send()
         gbq_copy(k).wait_send()
@@ -448,6 +470,8 @@
             pltpu.VMEM((no, rank, part), bf),
             pltpu.VMEM((no, ni) + share, bf),
             pltpu.VMEM((no, ni) + share, bf),
+            pltpu.VMEM((no, ni // 2) + share, bf),
+            pltpu.VMEM((no, ni) + share, bf),
             pltpu.VMEM((no,) + share, bf),
             pltpu.VMEM((no,) + share, bf),
             pltpu.VMEM((ni,) + share, bf),
@@ -460,7 +484,7 @@
             dma((3 + 2 * ni,)),
             dma((no,)), dma((no, ni)), dma((no, ni // 2)), dma((no, ni // 2)),
             dma((plane,)), dma((plane,)), dma((no,)), dma((no,)),
-            dma((no, ni)), dma((no, ni)),
+            dma((no, ni // 2)), dma((no, ni)), dma((no, ni // 2)), dma((no, ni)),
             dma((no,)), dma((no,)),
             dma((ni,)), dma((ni,)),
             dma((ni,)), dma((ni,)), dma((no,)), dma((no,)),

time: 34.7 us -> 34.1 us (0.983)
  Pallas kernels: 33.8 us -> 33.2 us
    pallas_call x1, Pallas kernels: 33.1 us -> 32.5 us  [on_device(): pl.pallas_call(functools.partial(kernel, (nh, no, ni, heads)), out_shape=...]
where the time goes in v3:
time: 34.1 us; the launch traced here: 33.9 us
  Pallas kernels  33.2 us (97%)
  between operations  0.64 us (2%)
    pallas_call x1, Pallas kernels, on_device(): pl.pallas_call(functools.partial(kernel, (nh, no, ni, heads)), out_shape=...  32.5 us
    pallas_call x1, Pallas kernels, on_device(): pl.pallas_call(put_out, out_shape=tuple((jax.ShapeDtypeStruct(*result) fo...  0.76 us

profile of v3, /device:TPU:0, one launch (start us, length us, event | category | flops | bytes accessed | tf_op | source)
XLA Modules:
  0.0 33.9 jit_solution(9666299036146617261)
XLA Ops:
  0.6 32.5 %shard_map.128 = (bf16[256,256]{1,0:T(8,128)(2,1)S(1)}, bf16[256,128]{1,0:T(8,128)(2,1)S(1)}, bf16[256,128]{1,0:T(8,128)(2,1)S(1)}, f32[16,1024]{1,0:T(8,128)S(1)}, f32[16,128]{1,0:T(8,128)S(1)}) custom-call(s32[8]{0:T(128)} %order_ref.1, s32[8,128]{1,0:T(8,128)} %bitcast.4, bf16[256,256]{1,0:T(8,128)(2,1)} %q_hbm.1, bf16[256,128]{1,0:T(8,128)(2,1)} %k_hbm.1, ...), custom_call_target="tpu_custom_call" | custom-call | tf_op jit(solution)/shard_map/pallas_call | solution.py:453
  33.1 0.8 %shard_map.129 = (bf16[256,256]{1,0:T(8,128)(2,1)}, bf16[256,128]{1,0:T(8,128)(2,1)}, bf16[256,128]{1,0:T(8,128)(2,1)}, f32[16,1024]{1,0:T(8,128)}, f32[16,128]{1,0:T(8,128)}) custom-call(bf16[256,256]{1,0:T(8,128)(2,1)S(1)} %get-tuple-element.15.refs_0_, bf16[256,128]{1,0:T(8,128)(2,1)S(1)} %get-tuple-element.16.refs_1_, ...), custom_call_target="tpu_custom_call" | custom-call | tf_op jit(solution)/shard_map/pallas_call | solution.py:499
